TPU v7x, 32 devices: a whole 2x2x4 slice. The times are simulated.
32 devices in a mesh: ctx: 8 (over z, y), tp: 4 (over x, core).
Axes of the slice: x: 2, y: 2, z: 4, core: 2. Of those that a mesh axis runs over, the one named last changes fastest.
Arguments:
- queries: bfloat16 [2048, 64, 128], P('ctx', 'tp'), may hold values from -48 to 48
- keys: bfloat16 [2048, 8, 128], P('ctx', 'tp'), may hold values from -3 to 3
- values: bfloat16 [2048, 8, 128], P('ctx', 'tp'), may hold values from -6 to 6
- segment_ids: int32 [2048], P('ctx'), may hold values from 0 to 7, never falling along the last dimension, each value on 1 to 1280 neighbouring positions
Outputs:
- attended: bfloat16 [2048, 8192], P(('ctx', 'tp'))
Inputs may be any that keep to these rules, and one draw needn't show every extreme that they name: `segment_ids`: ids never fall along the tokens; each document holds 1 to 1280 tokens, and one holds exactly 1280.
All inputs are finite; a program needn't handle non-finite values.
Results may differ from a plain program's by a relative error of at most 0.003.
Values may be sent and summed in bfloat16 or wider, within the bound.
A program may use at most 64 MiB of HBM per device.

v0:
```python
import math
import jax
import jax.numpy as jnp
from jax import lax
from jax.sharding import PartitionSpec as P


def passed_along(value, axis, by):
    length = lax.axis_size(axis)
    pairs = [(i, i + by) for i in range(length) if 0 <= i + by < length]
    return lax.ppermute(value, axis, pairs)


def attend_rows(state, grouped, seg_q, pos_q, keys, values, seg_k, pos_k, live):
    scale = 1.0 / math.sqrt(grouped.shape[-1])
    high, total, accum = state
    scores = jnp.einsum("tkgd,pkd->kgtp", grouped, keys, preferred_element_type=jnp.float32) * scale
    allowed = (seg_q[:, None] == seg_k[None, :]) & (pos_k[None, :] <= pos_q[:, None]) & live
    scores = jnp.where(allowed, scores, -1e30)
    newtop = jnp.maximum(high, jnp.max(scores, axis=-1))
    factor = jnp.exp(high - newtop)
    weights = jnp.where(allowed, jnp.exp(scores - newtop[..., None]), 0.0)
    total = total * factor + jnp.sum(weights, axis=-1)
    accum = accum * factor[..., None] + jnp.einsum(
        "kgtp,pkd->kgtd", weights.astype(jnp.bfloat16), values, preferred_element_type=jnp.float32
    )
    return (newtop, total, accum)


def fold_piece(state, grouped, seg_q, pos_q, keys, values, seg_k, start, live):
    length = keys.shape[0]
    first = 0 * length
    pos_rows = start + first + lax.iota(jnp.int32, length)
    return attend_rows(state, grouped, seg_q, pos_q, keys, values, seg_k, pos_rows, live)


def local(queries, keys, values, segment_ids):
    rows, heads, head = queries.shape
    groups = keys.shape[1]
    per_group = heads // groups
    ctx_count = lax.axis_size("ctx")
    here = lax.axis_index("ctx")
    grouped = queries.reshape(rows, groups, per_group, head)
    pos_q = here * rows + lax.iota(jnp.int32, rows)
    initial = (
        jnp.full((groups, per_group, rows), -1e30, jnp.float32),
        jnp.zeros((groups, per_group, rows), jnp.float32),
        jnp.zeros((groups, per_group, rows, head), jnp.float32),
    )
    longest = rows * ctx_count * 5 // 8
    reach = min((longest + rows - 1) // rows, ctx_count - 1)
    state = fold_piece(
        initial, grouped, segment_ids, pos_q, keys, values, segment_ids, here * rows, True
    )

    def step(distance, carry):
        state, block = carry
        block = passed_along((block[0], block[1], block[2]), "ctx", 1)
        owner = here - distance
        state = fold_piece(
            state,
            grouped,
            segment_ids,
            pos_q,
            block[0],
            block[1],
            block[2],
            owner * rows,
            owner >= 0,
        )
        return (state, block)

    state, unused = lax.fori_loop(1, reach + 1, step, (state, (keys, values, segment_ids)))
    high, total, accum = state
    result = (accum / total[..., None]).astype(jnp.bfloat16)
    result = jnp.transpose(result, (2, 0, 1, 3)).reshape(rows, heads * head)
    return lax.all_to_all(result, "tp", split_axis=0, concat_axis=1, tiled=True)


def solution(mesh):
    in_specs = (P("ctx", "tp", None), P("ctx", "tp", None), P("ctx", "tp", None), P("ctx"))
    out_specs = P(("ctx", "tp"), None)
    return jax.shard_map(local, mesh=mesh, in_specs=in_specs, out_specs=out_specs, check_vma=False)
```

profile of v0, /device:TPU:0, one launch (start us, length us, event | category | flops | bytes accessed | tf_op | source)
XLA Modules:
  0.0 117.8 jit_solution(8736475935258747422)
XLA Ops:
  1.6 1.5 %copy.21 = bf16[256,16,128]{2,0,1:T(8,128)(2,1)S(1)} copy(bf16[256,16,128]{2,1,0:T(8,128)(2,1)} %param.6) | data formatting | bytes 2097152 | tf_op args[0]
  3.1 1.6 %copy.25 = bf16[256,2,128]{2,0,1:T(8,128)(2,1)} copy(bf16[256,2,128]{2,1,0:T(2,128)(2,1)} %param.7) | data formatting | bytes 262144
  4.7 1.7 %fusion.20 = (f32[2,8,256]{2,1,0:T(8,128)S(1)}, f32[2,256,256,8]{2,1,3,0:T(8,128)S(1)}) fusion(pred[256,256]{0,1:T(8,128)(4,1)S(1)} %compare_and_fusion, bf16[256,2,8,128]{3,0,2,1:T(8,128)(2,1)S(1)} %bitcast.62, bf16[256,2,128,1]{2,1,0,3:T(2,128)(2,1)} %bitcast.65), kind=kOutput, calls=%fused_computation.26 | convolution fusion | flops 271577088 | bytes 5455872 | tf_op jit(solution)/shard_map/tkgd,pkd->kgtp/dot_general | solution.py:17
  6.4 1.9 %copy-done = f32[2,256,256,8]{2,1,3,0:T(8,128)} copy-done((f32[2,256,256,8]{2,1,3,0:T(8,128)}, f32[2,256,256,8]{2,1,3,0:T(8,128)S(1)}, u32[]{:S(2)}) %copy-start) | copy-done | bytes 4194328
  10.1 3.4 %fusion.30 = f32[2,8,256,128]{3,2,1,0:T(8,128)S(1)} fusion(f32[2,256,256,8]{2,1,3,0:T(8,128)} %copy-done, f32[2,8,256]{2,1,0:T(8,128)S(1)} %broadcast_maximum_fusion, pred[256,256]{0,1:T(8,128)(4,1)S(1)} %compare_and_fusion, f32[2,8,256]{2,1,0:T(8,128)S(1)} %get-tuple-element.278, bf16[256,2,128,1]{2,1,0,3:T(2,128)(2,1)S(1)} %bitcast.66), kind=kOutput, calls=%fused_computation.36 | convolution fusion | flops 274202624 | bytes 6520832 | tf_op jit(solution)/shard_map/kgtp,pkd->kgtd/dot_general | solution.py:24
  13.5 84.3 %while.24 = (s32[]{:T(128)}, f32[2,8,256]{2,1,0:T(8,128)S(1)}, f32[2,8,256]{2,1,0:T(8,128)S(1)}, f32[2,8,256,128]{3,2,1,0:T(8,128)S(1)}, bf16[256,2,128]{2,0,1:T...) while((s32[]{:T(128)}, f32[2,8,256]{2,1,0:T(8,128)S(1)}, ...), condition=%wide.region_5.6_spmd.clone, body=%wide.region_2.5_spmd.clone.sunk | while | flops 551821824 | bytes 20197672 | solution.py:73
  13.5 4.9 %collective-permute-start = (s32[256]{0:T(256)S(1)}, s32[256]{0:T(256)S(1)}, u32[]{:S(2)}, u32[]{:S(2)}) collective-permute-start(s32[256]{0:T(256)S(1)} %get-tuple-element.381), channel_id=1, source_target_pairs={{0,4},{4,8},{8,12},{12,16},{16,20},{20,24},{24,28},{1,5},{5,9},{9,... | collective-permute-start | bytes 3080 | tf_op jit(solution)/shard_map/while/body/eval_jaxpr/ppermute | solution.py:11
  18.4 3.4 %collective-permute-start.1 = (bf16[256,2,128]{2,0,1:T(8,128)(2,1)}, bf16[256,2,128]{2,0,1:T(8,128)(2,1)S(1)}, u32[]{:S(2)}, u32[]{:S(2)}) collective-permute-start(bf16[256,2,128]{2,0,1:T(8,128)(2,1)} %get-tuple-element.379), channel_id=1, source_target_pairs={{0,4},{4,8},{8,12},{12,16},{16,20},{20,24},{24,28},{1,5},{5,9},{9,... | collective-permute-start | bytes 393224 | tf_op jit(solution)/shard_map/while/body/eval_jaxpr/ppermute | solution.py:11
  21.9 3.4 %collective-permute-start.2 = (bf16[256,2,128]{2,0,1:T(8,128)(2,1)}, bf16[256,2,128]{2,0,1:T(8,128)(2,1)S(1)}, u32[]{:S(2)}, u32[]{:S(2)}) collective-permute-start(bf16[256,2,128]{2,0,1:T(8,128)(2,1)} %get-tuple-element.380), channel_id=1, source_target_pairs={{0,4},{4,8},{8,12},{12,16},{16,20},{20,24},{24,28},{1,5},{5,9},{9,... | collective-permute-start | bytes 393224 | tf_op jit(solution)/shard_map/while/body/eval_jaxpr/ppermute | solution.py:11
  26.3 1.0 fusion.52
  28.8 1.9 %multiply_add_fusion.5 = f32[2,8,256,128]{3,2,1,0:T(8,128)S(1)} fusion(f32[2,8,256,128]{3,2,1,0:T(8,128)S(1)} %get-tuple-element.378, f32[2,256,256,8]{2,1,3,0:T(8,128)S(1)} %get-tuple-element.358, f32[2,8,256]{2,1,0:T(8,128)S(1)} %max.9, pred[256,256]{0,1:T(8,128)(4,1)S(1)} %and_and_fusion.2, f32[2,8,256]{2,1,0:T(8,128)S(1)} %get-tuple-element.360, ...), kind=kOutput, calls=%fused_computation.7.clone.1 | convolution fusion | flops 274726912 | bytes 8617984 | tf_op jit(solution)/shard_map/while/body/eval_jaxpr/kgtp,pkd->kgtd/dot_general | solution.py:24
  30.6 4.2 %collective-permute-start = (s32[256]{0:T(256)S(1)}, s32[256]{0:T(256)S(1)}, u32[]{:S(2)}, u32[]{:S(2)}) collective-permute-start(s32[256]{0:T(256)S(1)} %get-tuple-element.381), channel_id=1, source_target_pairs={{0,4},{4,8},{8,12},{12,16},{16,20},{20,24},{24,28},{1,5},{5,9},{9,... | collective-permute-start | bytes 3080 | tf_op jit(solution)/shard_map/while/body/eval_jaxpr/ppermute | solution.py:11
  34.9 4.3 %collective-permute-start.1 = (bf16[256,2,128]{2,0,1:T(8,128)(2,1)}, bf16[256,2,128]{2,0,1:T(8,128)(2,1)S(1)}, u32[]{:S(2)}, u32[]{:S(2)}) collective-permute-start(bf16[256,2,128]{2,0,1:T(8,128)(2,1)} %get-tuple-element.379), channel_id=1, source_target_pairs={{0,4},{4,8},{8,12},{12,16},{16,20},{20,24},{24,28},{1,5},{5,9},{9,... | collective-permute-start | bytes 393224 | tf_op jit(solution)/shard_map/while/body/eval_jaxpr/ppermute | solution.py:11
  39.2 2.5 %collective-permute-start.2 = (bf16[256,2,128]{2,0,1:T(8,128)(2,1)}, bf16[256,2,128]{2,0,1:T(8,128)(2,1)S(1)}, u32[]{:S(2)}, u32[]{:S(2)}) collective-permute-start(bf16[256,2,128]{2,0,1:T(8,128)(2,1)} %get-tuple-element.380), channel_id=1, source_target_pairs={{0,4},{4,8},{8,12},{12,16},{16,20},{20,24},{24,28},{1,5},{5,9},{9,... | collective-permute-start | bytes 393224 | tf_op jit(solution)/shard_map/while/body/eval_jaxpr/ppermute | solution.py:11
  43.3 1.0 fusion.52
  45.7 1.9 %multiply_add_fusion.5 = f32[2,8,256,128]{3,2,1,0:T(8,128)S(1)} fusion(f32[2,8,256,128]{3,2,1,0:T(8,128)S(1)} %get-tuple-element.378, f32[2,256,256,8]{2,1,3,0:T(8,128)S(1)} %get-tuple-element.358, f32[2,8,256]{2,1,0:T(8,128)S(1)} %max.9, pred[256,256]{0,1:T(8,128)(4,1)S(1)} %and_and_fusion.2, f32[2,8,256]{2,1,0:T(8,128)S(1)} %get-tuple-element.360, ...), kind=kOutput, calls=%fused_computation.7.clone.1 | convolution fusion | flops 274726912 | bytes 8617984 | tf_op jit(solution)/shard_map/while/body/eval_jaxpr/kgtp,pkd->kgtd/dot_general | solution.py:24
  47.6 4.3 %collective-permute-start = (s32[256]{0:T(256)S(1)}, s32[256]{0:T(256)S(1)}, u32[]{:S(2)}, u32[]{:S(2)}) collective-permute-start(s32[256]{0:T(256)S(1)} %get-tuple-element.381), channel_id=1, source_target_pairs={{0,4},{4,8},{8,12},{12,16},{16,20},{20,24},{24,28},{1,5},{5,9},{9,... | collective-permute-start | bytes 3080 | tf_op jit(solution)/shard_map/while/body/eval_jaxpr/ppermute | solution.py:11
  51.9 4.7 %collective-permute-start.1 = (bf16[256,2,128]{2,0,1:T(8,128)(2,1)}, bf16[256,2,128]{2,0,1:T(8,128)(2,1)S(1)}, u32[]{:S(2)}, u32[]{:S(2)}) collective-permute-start(bf16[256,2,128]{2,0,1:T(8,128)(2,1)} %get-tuple-element.379), channel_id=1, source_target_pairs={{0,4},{4,8},{8,12},{12,16},{16,20},{20,24},{24,28},{1,5},{5,9},{9,... | collective-permute-start | bytes 393224 | tf_op jit(solution)/shard_map/while/body/eval_jaxpr/ppermute | solution.py:11
  56.6 2.1 %collective-permute-start.2 = (bf16[256,2,128]{2,0,1:T(8,128)(2,1)}, bf16[256,2,128]{2,0,1:T(8,128)(2,1)S(1)}, u32[]{:S(2)}, u32[]{:S(2)}) collective-permute-start(bf16[256,2,128]{2,0,1:T(8,128)(2,1)} %get-tuple-element.380), channel_id=1, source_target_pairs={{0,4},{4,8},{8,12},{12,16},{16,20},{20,24},{24,28},{1,5},{5,9},{9,... | collective-permute-start | bytes 393224 | tf_op jit(solution)/shard_map/while/body/eval_jaxpr/ppermute | solution.py:11
  60.2 1.0 fusion.52
  62.6 1.9 %multiply_add_fusion.5 = f32[2,8,256,128]{3,2,1,0:T(8,128)S(1)} fusion(f32[2,8,256,128]{3,2,1,0:T(8,128)S(1)} %get-tuple-element.378, f32[2,256,256,8]{2,1,3,0:T(8,128)S(1)} %get-tuple-element.358, f32[2,8,256]{2,1,0:T(8,128)S(1)} %max.9, pred[256,256]{0,1:T(8,128)(4,1)S(1)} %and_and_fusion.2, f32[2,8,256]{2,1,0:T(8,128)S(1)} %get-tuple-element.360, ...), kind=kOutput, calls=%fused_computation.7.clone.1 | convolution fusion | flops 274726912 | bytes 8617984 | tf_op jit(solution)/shard_map/while/body/eval_jaxpr/kgtp,pkd->kgtd/dot_general | solution.py:24
  64.5 4.3 %collective-permute-start = (s32[256]{0:T(256)S(1)}, s32[256]{0:T(256)S(1)}, u32[]{:S(2)}, u32[]{:S(2)}) collective-permute-start(s32[256]{0:T(256)S(1)} %get-tuple-element.381), channel_id=1, source_target_pairs={{0,4},{4,8},{8,12},{12,16},{16,20},{20,24},{24,28},{1,5},{5,9},{9,... | collective-permute-start | bytes 3080 | tf_op jit(solution)/shard_map/while/body/eval_jaxpr/ppermute | solution.py:11
  68.8 5.2 %collective-permute-start.1 = (bf16[256,2,128]{2,0,1:T(8,128)(2,1)}, bf16[256,2,128]{2,0,1:T(8,128)(2,1)S(1)}, u32[]{:S(2)}, u32[]{:S(2)}) collective-permute-start(bf16[256,2,128]{2,0,1:T(8,128)(2,1)} %get-tuple-element.379), channel_id=1, source_target_pairs={{0,4},{4,8},{8,12},{12,16},{16,20},{20,24},{24,28},{1,5},{5,9},{9,... | collective-permute-start | bytes 393224 | tf_op jit(solution)/shard_map/while/body/eval_jaxpr/ppermute | solution.py:11
  74.0 1.9 %collective-permute-start.2 = (bf16[256,2,128]{2,0,1:T(8,128)(2,1)}, bf16[256,2,128]{2,0,1:T(8,128)(2,1)S(1)}, u32[]{:S(2)}, u32[]{:S(2)}) collective-permute-start(bf16[256,2,128]{2,0,1:T(8,128)(2,1)} %get-tuple-element.380), channel_id=1, source_target_pairs={{0,4},{4,8},{8,12},{12,16},{16,20},{20,24},{24,28},{1,5},{5,9},{9,... | collective-permute-start | bytes 393224 | tf_op jit(solution)/shard_map/while/body/eval_jaxpr/ppermute | solution.py:11
  77.6 1.0 fusion.52
  79.9 1.9 %multiply_add_fusion.5 = f32[2,8,256,128]{3,2,1,0:T(8,128)S(1)} fusion(f32[2,8,256,128]{3,2,1,0:T(8,128)S(1)} %get-tuple-element.378, f32[2,256,256,8]{2,1,3,0:T(8,128)S(1)} %get-tuple-element.358, f32[2,8,256]{2,1,0:T(8,128)S(1)} %max.9, pred[256,256]{0,1:T(8,128)(4,1)S(1)} %and_and_fusion.2, f32[2,8,256]{2,1,0:T(8,128)S(1)} %get-tuple-element.360, ...), kind=kOutput, calls=%fused_computation.7.clone.1 | convolution fusion | flops 274726912 | bytes 8617984 | tf_op jit(solution)/shard_map/while/body/eval_jaxpr/kgtp,pkd->kgtd/dot_general | solution.py:24
  81.8 4.2 %collective-permute-start = (s32[256]{0:T(256)S(1)}, s32[256]{0:T(256)S(1)}, u32[]{:S(2)}, u32[]{:S(2)}) collective-permute-start(s32[256]{0:T(256)S(1)} %get-tuple-element.381), channel_id=1, source_target_pairs={{0,4},{4,8},{8,12},{12,16},{16,20},{20,24},{24,28},{1,5},{5,9},{9,... | collective-permute-start | bytes 3080 | tf_op jit(solution)/shard_map/while/body/eval_jaxpr/ppermute | solution.py:11
  86.1 3.8 %collective-permute-start.1 = (bf16[256,2,128]{2,0,1:T(8,128)(2,1)}, bf16[256,2,128]{2,0,1:T(8,128)(2,1)S(1)}, u32[]{:S(2)}, u32[]{:S(2)}) collective-permute-start(bf16[256,2,128]{2,0,1:T(8,128)(2,1)} %get-tuple-element.379), channel_id=1, source_target_pairs={{0,4},{4,8},{8,12},{12,16},{16,20},{20,24},{24,28},{1,5},{5,9},{9,... | collective-permute-start | bytes 393224 | tf_op jit(solution)/shard_map/while/body/eval_jaxpr/ppermute | solution.py:11
  89.9 1.9 %collective-permute-start.2 = (bf16[256,2,128]{2,0,1:T(8,128)(2,1)}, bf16[256,2,128]{2,0,1:T(8,128)(2,1)S(1)}, u32[]{:S(2)}, u32[]{:S(2)}) collective-permute-start(bf16[256,2,128]{2,0,1:T(8,128)(2,1)} %get-tuple-element.380), channel_id=1, source_target_pairs={{0,4},{4,8},{8,12},{12,16},{16,20},{20,24},{24,28},{1,5},{5,9},{9,... | collective-permute-start | bytes 393224 | tf_op jit(solution)/shard_map/while/body/eval_jaxpr/ppermute | solution.py:11
  95.9 1.9 %multiply_add_fusion.5 = f32[2,8,256,128]{3,2,1,0:T(8,128)S(1)} fusion(f32[2,8,256,128]{3,2,1,0:T(8,128)S(1)} %get-tuple-element.378, f32[2,256,256,8]{2,1,3,0:T(8,128)S(1)} %get-tuple-element.358, f32[2,8,256]{2,1,0:T(8,128)S(1)} %max.9, pred[256,256]{0,1:T(8,128)(4,1)S(1)} %and_and_fusion.2, f32[2,8,256]{2,1,0:T(8,128)S(1)} %get-tuple-element.360, ...), kind=kOutput, calls=%fused_computation.7.clone.1 | convolution fusion | flops 274726912 | bytes 8617984 | tf_op jit(solution)/shard_map/while/body/eval_jaxpr/kgtp,pkd->kgtd/dot_general | solution.py:24
  99.7 17.0 %all_to_all.19 = bf16[4,64,2048]{2,1,0:T(8,128)(2,1)S(1)} all-to-all(bf16[4,64,2048]{2,1,0:T(8,128)(2,1)S(1)} %all_to_all.14), channel_id=1, replica_groups=mesh['ctx'=8,'tp'=4] {'tp'}, dimensions={0} | all-to-all | bytes 2097152 | tf_op jit(solution)/shard_map/all_to_all | solution.py:77
  116.7 1.1 copy.39
  (76 shorter events, 20.0 us)
Async XLA Ops:
  4.7 4.7 %copy-start.1 = (bf16[256,2,128]{2,1,0:T(2,128)(2,1)S(1)}, bf16[256,2,128]{2,1,0:T(2,128)(2,1)}, u32[]{:S(2)}) copy-start(bf16[256,2,128]{2,1,0:T(2,128)(2,1)} %param.8) | copy-start | bytes 393220
  6.4 1.9 %copy-start = (f32[2,256,256,8]{2,1,3,0:T(8,128)}, f32[2,256,256,8]{2,1,3,0:T(8,128)S(1)}, u32[]{:S(2)}) copy-start(f32[2,256,256,8]{2,1,3,0:T(8,128)S(1)} %get-tuple-element.281) | copy-start | bytes 12582916
  10.1 3.4 %copy-start.2 = (s32[256]{0:T(256)S(1)}, s32[256]{0:T(256)}, u32[]{:S(2)}) copy-start(s32[256]{0:T(256)} %param.9) | copy-start | bytes 3076
  13.5 11.8 %collective-permute-start = (s32[256]{0:T(256)S(1)}, s32[256]{0:T(256)S(1)}, u32[]{:S(2)}, u32[]{:S(2)}) collective-permute-start(s32[256]{0:T(256)S(1)} %get-tuple-element.381), channel_id=1, source_target_pairs={{0,4},{4,8},{8,12},{12,16},{16,20},{20,24},{24,28},{1,5},{5,9},{9,... | collective-permute-start | bytes 3080 | tf_op jit(solution)/shard_map/while/body/eval_jaxpr/ppermute | solution.py:11
  18.4 7.1 %collective-permute-start.1 = (bf16[256,2,128]{2,0,1:T(8,128)(2,1)}, bf16[256,2,128]{2,0,1:T(8,128)(2,1)S(1)}, u32[]{:S(2)}, u32[]{:S(2)}) collective-permute-start(bf16[256,2,128]{2,0,1:T(8,128)(2,1)} %get-tuple-element.379), channel_id=1, source_target_pairs={{0,4},{4,8},{8,12},{12,16},{16,20},{20,24},{24,28},{1,5},{5,9},{9,... | collective-permute-start | bytes 393224 | tf_op jit(solution)/shard_map/while/body/eval_jaxpr/ppermute | solution.py:11
  21.9 6.2 %collective-permute-start.2 = (bf16[256,2,128]{2,0,1:T(8,128)(2,1)}, bf16[256,2,128]{2,0,1:T(8,128)(2,1)S(1)}, u32[]{:S(2)}, u32[]{:S(2)}) collective-permute-start(bf16[256,2,128]{2,0,1:T(8,128)(2,1)} %get-tuple-element.380), channel_id=1, source_target_pairs={{0,4},{4,8},{8,12},{12,16},{16,20},{20,24},{24,28},{1,5},{5,9},{9,... | collective-permute-start | bytes 393224 | tf_op jit(solution)/shard_map/while/body/eval_jaxpr/ppermute | solution.py:11
  30.6 11.2 %collective-permute-start = (s32[256]{0:T(256)S(1)}, s32[256]{0:T(256)S(1)}, u32[]{:S(2)}, u32[]{:S(2)}) collective-permute-start(s32[256]{0:T(256)S(1)} %get-tuple-element.381), channel_id=1, source_target_pairs={{0,4},{4,8},{8,12},{12,16},{16,20},{20,24},{24,28},{1,5},{5,9},{9,... | collective-permute-start | bytes 3080 | tf_op jit(solution)/shard_map/while/body/eval_jaxpr/ppermute | solution.py:11
  34.9 7.7 %collective-permute-start.1 = (bf16[256,2,128]{2,0,1:T(8,128)(2,1)}, bf16[256,2,128]{2,0,1:T(8,128)(2,1)S(1)}, u32[]{:S(2)}, u32[]{:S(2)}) collective-permute-start(bf16[256,2,128]{2,0,1:T(8,128)(2,1)} %get-tuple-element.379), channel_id=1, source_target_pairs={{0,4},{4,8},{8,12},{12,16},{16,20},{20,24},{24,28},{1,5},{5,9},{9,... | collective-permute-start | bytes 393224 | tf_op jit(solution)/shard_map/while/body/eval_jaxpr/ppermute | solution.py:11
  39.2 5.8 %collective-permute-start.2 = (bf16[256,2,128]{2,0,1:T(8,128)(2,1)}, bf16[256,2,128]{2,0,1:T(8,128)(2,1)S(1)}, u32[]{:S(2)}, u32[]{:S(2)}) collective-permute-start(bf16[256,2,128]{2,0,1:T(8,128)(2,1)} %get-tuple-element.380), channel_id=1, source_target_pairs={{0,4},{4,8},{8,12},{12,16},{16,20},{20,24},{24,28},{1,5},{5,9},{9,... | collective-permute-start | bytes 393224 | tf_op jit(solution)/shard_map/while/body/eval_jaxpr/ppermute | solution.py:11
  47.6 11.2 %collective-permute-start = (s32[256]{0:T(256)S(1)}, s32[256]{0:T(256)S(1)}, u32[]{:S(2)}, u32[]{:S(2)}) collective-permute-start(s32[256]{0:T(256)S(1)} %get-tuple-element.381), channel_id=1, source_target_pairs={{0,4},{4,8},{8,12},{12,16},{16,20},{20,24},{24,28},{1,5},{5,9},{9,... | collective-permute-start | bytes 3080 | tf_op jit(solution)/shard_map/while/body/eval_jaxpr/ppermute | solution.py:11
  51.9 7.6 %collective-permute-start.1 = (bf16[256,2,128]{2,0,1:T(8,128)(2,1)}, bf16[256,2,128]{2,0,1:T(8,128)(2,1)S(1)}, u32[]{:S(2)}, u32[]{:S(2)}) collective-permute-start(bf16[256,2,128]{2,0,1:T(8,128)(2,1)} %get-tuple-element.379), channel_id=1, source_target_pairs={{0,4},{4,8},{8,12},{12,16},{16,20},{20,24},{24,28},{1,5},{5,9},{9,... | collective-permute-start | bytes 393224 | tf_op jit(solution)/shard_map/while/body/eval_jaxpr/ppermute | solution.py:11
  56.6 5.3 %collective-permute-start.2 = (bf16[256,2,128]{2,0,1:T(8,128)(2,1)}, bf16[256,2,128]{2,0,1:T(8,128)(2,1)S(1)}, u32[]{:S(2)}, u32[]{:S(2)}) collective-permute-start(bf16[256,2,128]{2,0,1:T(8,128)(2,1)} %get-tuple-element.380), channel_id=1, source_target_pairs={{0,4},{4,8},{8,12},{12,16},{16,20},{20,24},{24,28},{1,5},{5,9},{9,... | collective-permute-start | bytes 393224 | tf_op jit(solution)/shard_map/while/body/eval_jaxpr/ppermute | solution.py:11
  64.5 11.4 %collective-permute-start = (s32[256]{0:T(256)S(1)}, s32[256]{0:T(256)S(1)}, u32[]{:S(2)}, u32[]{:S(2)}) collective-permute-start(s32[256]{0:T(256)S(1)} %get-tuple-element.381), channel_id=1, source_target_pairs={{0,4},{4,8},{8,12},{12,16},{16,20},{20,24},{24,28},{1,5},{5,9},{9,... | collective-permute-start | bytes 3080 | tf_op jit(solution)/shard_map/while/body/eval_jaxpr/ppermute | solution.py:11
  68.8 8.0 %collective-permute-start.1 = (bf16[256,2,128]{2,0,1:T(8,128)(2,1)}, bf16[256,2,128]{2,0,1:T(8,128)(2,1)S(1)}, u32[]{:S(2)}, u32[]{:S(2)}) collective-permute-start(bf16[256,2,128]{2,0,1:T(8,128)(2,1)} %get-tuple-element.379), channel_id=1, source_target_pairs={{0,4},{4,8},{8,12},{12,16},{16,20},{20,24},{24,28},{1,5},{5,9},{9,... | collective-permute-start | bytes 393224 | tf_op jit(solution)/shard_map/while/body/eval_jaxpr/ppermute | solution.py:11
  74.0 5.3 %collective-permute-start.2 = (bf16[256,2,128]{2,0,1:T(8,128)(2,1)}, bf16[256,2,128]{2,0,1:T(8,128)(2,1)S(1)}, u32[]{:S(2)}, u32[]{:S(2)}) collective-permute-start(bf16[256,2,128]{2,0,1:T(8,128)(2,1)} %get-tuple-element.380), channel_id=1, source_target_pairs={{0,4},{4,8},{8,12},{12,16},{16,20},{20,24},{24,28},{1,5},{5,9},{9,... | collective-permute-start | bytes 393224 | tf_op jit(solution)/shard_map/while/body/eval_jaxpr/ppermute | solution.py:11
  81.8 10.0 %collective-permute-start = (s32[256]{0:T(256)S(1)}, s32[256]{0:T(256)S(1)}, u32[]{:S(2)}, u32[]{:S(2)}) collective-permute-start(s32[256]{0:T(256)S(1)} %get-tuple-element.381), channel_id=1, source_target_pairs={{0,4},{4,8},{8,12},{12,16},{16,20},{20,24},{24,28},{1,5},{5,9},{9,... | collective-permute-start | bytes 3080 | tf_op jit(solution)/shard_map/while/body/eval_jaxpr/ppermute | solution.py:11
  86.1 6.6 %collective-permute-start.1 = (bf16[256,2,128]{2,0,1:T(8,128)(2,1)}, bf16[256,2,128]{2,0,1:T(8,128)(2,1)S(1)}, u32[]{:S(2)}, u32[]{:S(2)}) collective-permute-start(bf16[256,2,128]{2,0,1:T(8,128)(2,1)} %get-tuple-element.379), channel_id=1, source_target_pairs={{0,4},{4,8},{8,12},{12,16},{16,20},{20,24},{24,28},{1,5},{5,9},{9,... | collective-permute-start | bytes 393224 | tf_op jit(solution)/shard_map/while/body/eval_jaxpr/ppermute | solution.py:11
  89.9 5.3 %collective-permute-start.2 = (bf16[256,2,128]{2,0,1:T(8,128)(2,1)}, bf16[256,2,128]{2,0,1:T(8,128)(2,1)S(1)}, u32[]{:S(2)}, u32[]{:S(2)}) collective-permute-start(bf16[256,2,128]{2,0,1:T(8,128)(2,1)} %get-tuple-element.380), channel_id=1, source_target_pairs={{0,4},{4,8},{8,12},{12,16},{16,20},{20,24},{24,28},{1,5},{5,9},{9,... | collective-permute-start | bytes 393224 | tf_op jit(solution)/shard_map/while/body/eval_jaxpr/ppermute | solution.py:11
where the time goes:
time: 118 us
  starting transfers between devices  55.4 us (47%)
  matrix products  18.3 us (16%)
  blocking collectives  17 us (14%)
  local copies, waits for them, and re-layouts  15.2 us (13%)
  other arithmetic  8.57 us (7%)
  waiting for transfers between devices  2.57 us (2%)
    ppermute x15, starting transfers between devices, passed_along(): return lax.ppermute(value, axis, pairs)  55.4 us
    all_to_all x1, blocking collectives, local(): return lax.all_to_all(result, 'tp', split_axis=0, concat_axis=1, tiled=True)  17 us
    dot_general x6, matrix products, attend_rows(): jnp.einsum('kgtp,pkd->kgtd', weights.astype(jnp.bfloat16), values, prefer...  12.8 us
    while x20, local copies, waits for them, and re-layouts  6.59 us
    unnamed x10, local copies, waits for them, and re-layouts  6.36 us
    reduce_sum x6, other arithmetic, attend_rows(): total = total * factor + jnp.sum(weights, axis=-1)  6.12 us
    dot_general x6, matrix products, attend_rows(): jnp.einsum('tkgd,pkd->kgtp', grouped, keys, preferred_element_type=jnp.fl...  5.53 us
    ppermute x15, waiting for transfers between devices, passed_along(): return lax.ppermute(value, axis, pairs)  2.57 us
  transfers between devices with their start and end apart: 15, of which 5 were waited for; matrix products, arithmetic and copies ran while one was open for 11% of the time, Pallas kernels for 0%

commit v1 on v0

--- a/solution.py
+++ b/solution.py
@@ -74,7 +74,10 @@
     high, total, accum = state
     result = (accum / total[..., None]).astype(jnp.bfloat16)
     result = jnp.transpose(result, (2, 0, 1, 3)).reshape(rows, heads * head)
-    return lax.all_to_all(result, "tp", split_axis=0, concat_axis=1, tiled=True)
+    return jnp.concatenate(
+        lax.all_to_all(jnp.stack(jnp.split(result, lax.axis_size("tp"), axis=0)), "tp", 0, 0),
+        axis=1,
+    )
 
 
 def solution(mesh):

time: 118 us -> 119 us (level)
    all_to_all x2 -> x0, local copies, waits for them, and re-layouts: 1.57 us -> none  [local(): return lax.all_to_all(result, 'tp', split_axis=0, concat_axis=1, tiled=True)]
where the time goes in v1:
time: 119 us; the launch traced here: 118 us
  starting transfers between devices  55.4 us (47%)
  matrix products  18.3 us (15%)
  blocking collectives  17 us (14%)
  local copies, waits for them, and re-layouts  15.1 us (13%)
  other arithmetic  8.71 us (7%)
  waiting for transfers between devices  2.57 us (2%)
    ppermute x15, starting transfers between devices, passed_along(): return lax.ppermute(value, axis, pairs)  55.4 us
    all_to_all x1, blocking collectives, local(): lax.all_to_all(jnp.stack(jnp.split(result, lax.axis_size('tp'), axis=0)),...  17 us
    dot_general x6, matrix products, attend_rows(): jnp.einsum('kgtp,pkd->kgtd', weights.astype(jnp.bfloat16), values, prefer...  12.8 us
    while x20, local copies, waits for them, and re-layouts  6.52 us
    unnamed x10, local copies, waits for them, and re-layouts  6.34 us
    reduce_sum x6, other arithmetic, attend_rows(): total = total * factor + jnp.sum(weights, axis=-1)  6.12 us
    dot_general x6, matrix products, attend_rows(): jnp.einsum('tkgd,pkd->kgtp', grouped, keys, preferred_element_type=jnp.fl...  5.53 us
    ppermute x15, waiting for transfers between devices, passed_along(): return lax.ppermute(value, axis, pairs)  2.57 us
  transfers between devices with their start and end apart: 15, of which 5 were waited for; matrix products, arithmetic and copies ran while one was open for 11% of the time, Pallas kernels for 0%

profile of v1, /device:TPU:0, one launch (start us, length us, event | category | flops | bytes accessed | tf_op | source)
XLA Modules:
  0.0 117.9 jit_solution(1158239947586649523)
XLA Ops:
  1.6 1.5 %copy.24 = bf16[256,16,128]{2,0,1:T(8,128)(2,1)S(1)} copy(bf16[256,16,128]{2,1,0:T(8,128)(2,1)} %param.6) | data formatting | bytes 2097152 | tf_op args[0]
  3.1 1.6 %copy.28 = bf16[256,2,128]{2,0,1:T(8,128)(2,1)} copy(bf16[256,2,128]{2,1,0:T(2,128)(2,1)} %param.7) | data formatting | bytes 262144
  4.7 1.7 %fusion.20 = (f32[2,8,256]{2,1,0:T(8,128)S(1)}, f32[2,256,256,8]{2,1,3,0:T(8,128)S(1)}) fusion(pred[256,256]{0,1:T(8,128)(4,1)S(1)} %compare_and_fusion, bf16[256,2,8,128]{3,0,2,1:T(8,128)(2,1)S(1)} %bitcast.68, bf16[256,2,128,1]{2,1,0,3:T(2,128)(2,1)} %bitcast.71), kind=kOutput, calls=%fused_computation.26 | convolution fusion | flops 271577088 | bytes 5455872 | tf_op jit(solution)/shard_map/tkgd,pkd->kgtp/dot_general | solution.py:17
  6.4 1.9 %copy-done = f32[2,256,256,8]{2,1,3,0:T(8,128)} copy-done((f32[2,256,256,8]{2,1,3,0:T(8,128)}, f32[2,256,256,8]{2,1,3,0:T(8,128)S(1)}, u32[]{:S(2)}) %copy-start) | copy-done | bytes 4194328
  10.0 3.4 %fusion.30 = f32[2,8,256,128]{3,2,1,0:T(8,128)S(1)} fusion(f32[2,256,256,8]{2,1,3,0:T(8,128)} %copy-done, f32[2,8,256]{2,1,0:T(8,128)S(1)} %broadcast_maximum_fusion, pred[256,256]{0,1:T(8,128)(4,1)S(1)} %compare_and_fusion, f32[2,8,256]{2,1,0:T(8,128)S(1)} %get-tuple-element.282, bf16[256,2,128,1]{2,1,0,3:T(2,128)(2,1)S(1)} %bitcast.72), kind=kOutput, calls=%fused_computation.36 | convolution fusion | flops 274202624 | bytes 6520832 | tf_op jit(solution)/shard_map/kgtp,pkd->kgtd/dot_general | solution.py:24
  13.5 84.2 %while.24 = (s32[]{:T(128)}, f32[2,8,256]{2,1,0:T(8,128)S(1)}, f32[2,8,256]{2,1,0:T(8,128)S(1)}, f32[2,8,256,128]{3,2,1,0:T(8,128)S(1)}, bf16[256,2,128]{2,0,1:T...) while((s32[]{:T(128)}, f32[2,8,256]{2,1,0:T(8,128)S(1)}, ...), condition=%wide.region_5.6_spmd.clone, body=%wide.region_2.5_spmd.clone.sunk | while | flops 551821824 | bytes 20197672 | solution.py:73
  13.5 4.9 %collective-permute-start = (s32[256]{0:T(256)S(1)}, s32[256]{0:T(256)S(1)}, u32[]{:S(2)}, u32[]{:S(2)}) collective-permute-start(s32[256]{0:T(256)S(1)} %get-tuple-element.385), channel_id=1, source_target_pairs={{0,4},{4,8},{8,12},{12,16},{16,20},{20,24},{24,28},{1,5},{5,9},{9,... | collective-permute-start | bytes 3080 | tf_op jit(solution)/shard_map/while/body/eval_jaxpr/ppermute | solution.py:11
  18.4 3.4 %collective-permute-start.1 = (bf16[256,2,128]{2,0,1:T(8,128)(2,1)}, bf16[256,2,128]{2,0,1:T(8,128)(2,1)S(1)}, u32[]{:S(2)}, u32[]{:S(2)}) collective-permute-start(bf16[256,2,128]{2,0,1:T(8,128)(2,1)} %get-tuple-element.383), channel_id=1, source_target_pairs={{0,4},{4,8},{8,12},{12,16},{16,20},{20,24},{24,28},{1,5},{5,9},{9,... | collective-permute-start | bytes 393224 | tf_op jit(solution)/shard_map/while/body/eval_jaxpr/ppermute | solution.py:11
  21.8 3.4 %collective-permute-start.2 = (bf16[256,2,128]{2,0,1:T(8,128)(2,1)}, bf16[256,2,128]{2,0,1:T(8,128)(2,1)S(1)}, u32[]{:S(2)}, u32[]{:S(2)}) collective-permute-start(bf16[256,2,128]{2,0,1:T(8,128)(2,1)} %get-tuple-element.384), channel_id=1, source_target_pairs={{0,4},{4,8},{8,12},{12,16},{16,20},{20,24},{24,28},{1,5},{5,9},{9,... | collective-permute-start | bytes 393224 | tf_op jit(solution)/shard_map/while/body/eval_jaxpr/ppermute | solution.py:11
  26.3 1.0 fusion.53
  28.7 1.9 %multiply_add_fusion.5 = f32[2,8,256,128]{3,2,1,0:T(8,128)S(1)} fusion(f32[2,8,256,128]{3,2,1,0:T(8,128)S(1)} %get-tuple-element.382, f32[2,256,256,8]{2,1,3,0:T(8,128)S(1)} %get-tuple-element.362, f32[2,8,256]{2,1,0:T(8,128)S(1)} %max.9, pred[256,256]{0,1:T(8,128)(4,1)S(1)} %and_and_fusion.2, f32[2,8,256]{2,1,0:T(8,128)S(1)} %get-tuple-element.364, ...), kind=kOutput, calls=%fused_computation.7.clone.1 | convolution fusion | flops 274726912 | bytes 8617984 | tf_op jit(solution)/shard_map/while/body/eval_jaxpr/kgtp,pkd->kgtd/dot_general | solution.py:24
  30.6 4.2 %collective-permute-start = (s32[256]{0:T(256)S(1)}, s32[256]{0:T(256)S(1)}, u32[]{:S(2)}, u32[]{:S(2)}) collective-permute-start(s32[256]{0:T(256)S(1)} %get-tuple-element.385), channel_id=1, source_target_pairs={{0,4},{4,8},{8,12},{12,16},{16,20},{20,24},{24,28},{1,5},{5,9},{9,... | collective-permute-start | bytes 3080 | tf_op jit(solution)/shard_map/while/body/eval_jaxpr/ppermute | solution.py:11
  34.9 4.3 %collective-permute-start.1 = (bf16[256,2,128]{2,0,1:T(8,128)(2,1)}, bf16[256,2,128]{2,0,1:T(8,128)(2,1)S(1)}, u32[]{:S(2)}, u32[]{:S(2)}) collective-permute-start(bf16[256,2,128]{2,0,1:T(8,128)(2,1)} %get-tuple-element.383), channel_id=1, source_target_pairs={{0,4},{4,8},{8,12},{12,16},{16,20},{20,24},{24,28},{1,5},{5,9},{9,... | collective-permute-start | bytes 393224 | tf_op jit(solution)/shard_map/while/body/eval_jaxpr/ppermute | solution.py:11
  39.2 2.5 %collective-permute-start.2 = (bf16[256,2,128]{2,0,1:T(8,128)(2,1)}, bf16[256,2,128]{2,0,1:T(8,128)(2,1)S(1)}, u32[]{:S(2)}, u32[]{:S(2)}) collective-permute-start(bf16[256,2,128]{2,0,1:T(8,128)(2,1)} %get-tuple-element.384), channel_id=1, source_target_pairs={{0,4},{4,8},{8,12},{12,16},{16,20},{20,24},{24,28},{1,5},{5,9},{9,... | collective-permute-start | bytes 393224 | tf_op jit(solution)/shard_map/while/body/eval_jaxpr/ppermute | solution.py:11
  43.3 1.0 fusion.53
  45.7 1.9 %multiply_add_fusion.5 = f32[2,8,256,128]{3,2,1,0:T(8,128)S(1)} fusion(f32[2,8,256,128]{3,2,1,0:T(8,128)S(1)} %get-tuple-element.382, f32[2,256,256,8]{2,1,3,0:T(8,128)S(1)} %get-tuple-element.362, f32[2,8,256]{2,1,0:T(8,128)S(1)} %max.9, pred[256,256]{0,1:T(8,128)(4,1)S(1)} %and_and_fusion.2, f32[2,8,256]{2,1,0:T(8,128)S(1)} %get-tuple-element.364, ...), kind=kOutput, calls=%fused_computation.7.clone.1 | convolution fusion | flops 274726912 | bytes 8617984 | tf_op jit(solution)/shard_map/while/body/eval_jaxpr/kgtp,pkd->kgtd/dot_general | solution.py:24
  47.6 4.3 %collective-permute-start = (s32[256]{0:T(256)S(1)}, s32[256]{0:T(256)S(1)}, u32[]{:S(2)}, u32[]{:S(2)}) collective-permute-start(s32[256]{0:T(256)S(1)} %get-tuple-element.385), channel_id=1, source_target_pairs={{0,4},{4,8},{8,12},{12,16},{16,20},{20,24},{24,28},{1,5},{5,9},{9,... | collective-permute-start | bytes 3080 | tf_op jit(solution)/shard_map/while/body/eval_jaxpr/ppermute | solution.py:11
  51.8 4.7 %collective-permute-start.1 = (bf16[256,2,128]{2,0,1:T(8,128)(2,1)}, bf16[256,2,128]{2,0,1:T(8,128)(2,1)S(1)}, u32[]{:S(2)}, u32[]{:S(2)}) collective-permute-start(bf16[256,2,128]{2,0,1:T(8,128)(2,1)} %get-tuple-element.383), channel_id=1, source_target_pairs={{0,4},{4,8},{8,12},{12,16},{16,20},{20,24},{24,28},{1,5},{5,9},{9,... | collective-permute-start | bytes 393224 | tf_op jit(solution)/shard_map/while/body/eval_jaxpr/ppermute | solution.py:11
  56.6 2.1 %collective-permute-start.2 = (bf16[256,2,128]{2,0,1:T(8,128)(2,1)}, bf16[256,2,128]{2,0,1:T(8,128)(2,1)S(1)}, u32[]{:S(2)}, u32[]{:S(2)}) collective-permute-start(bf16[256,2,128]{2,0,1:T(8,128)(2,1)} %get-tuple-element.384), channel_id=1, source_target_pairs={{0,4},{4,8},{8,12},{12,16},{16,20},{20,24},{24,28},{1,5},{5,9},{9,... | collective-permute-start | bytes 393224 | tf_op jit(solution)/shard_map/while/body/eval_jaxpr/ppermute | solution.py:11
  60.2 1.0 fusion.53
  62.5 1.9 %multiply_add_fusion.5 = f32[2,8,256,128]{3,2,1,0:T(8,128)S(1)} fusion(f32[2,8,256,128]{3,2,1,0:T(8,128)S(1)} %get-tuple-element.382, f32[2,256,256,8]{2,1,3,0:T(8,128)S(1)} %get-tuple-element.362, f32[2,8,256]{2,1,0:T(8,128)S(1)} %max.9, pred[256,256]{0,1:T(8,128)(4,1)S(1)} %and_and_fusion.2, f32[2,8,256]{2,1,0:T(8,128)S(1)} %get-tuple-element.364, ...), kind=kOutput, calls=%fused_computation.7.clone.1 | convolution fusion | flops 274726912 | bytes 8617984 | tf_op jit(solution)/shard_map/while/body/eval_jaxpr/kgtp,pkd->kgtd/dot_general | solution.py:24
  64.4 4.3 %collective-permute-start = (s32[256]{0:T(256)S(1)}, s32[256]{0:T(256)S(1)}, u32[]{:S(2)}, u32[]{:S(2)}) collective-permute-start(s32[256]{0:T(256)S(1)} %get-tuple-element.385), channel_id=1, source_target_pairs={{0,4},{4,8},{8,12},{12,16},{16,20},{20,24},{24,28},{1,5},{5,9},{9,... | collective-permute-start | bytes 3080 | tf_op jit(solution)/shard_map/while/body/eval_jaxpr/ppermute | solution.py:11
  68.7 5.2 %collective-permute-start.1 = (bf16[256,2,128]{2,0,1:T(8,128)(2,1)}, bf16[256,2,128]{2,0,1:T(8,128)(2,1)S(1)}, u32[]{:S(2)}, u32[]{:S(2)}) collective-permute-start(bf16[256,2,128]{2,0,1:T(8,128)(2,1)} %get-tuple-element.383), channel_id=1, source_target_pairs={{0,4},{4,8},{8,12},{12,16},{16,20},{20,24},{24,28},{1,5},{5,9},{9,... | collective-permute-start | bytes 393224 | tf_op jit(solution)/shard_map/while/body/eval_jaxpr/ppermute | solution.py:11
  73.9 1.9 %collective-permute-start.2 = (bf16[256,2,128]{2,0,1:T(8,128)(2,1)}, bf16[256,2,128]{2,0,1:T(8,128)(2,1)S(1)}, u32[]{:S(2)}, u32[]{:S(2)}) collective-permute-start(bf16[256,2,128]{2,0,1:T(8,128)(2,1)} %get-tuple-element.384), channel_id=1, source_target_pairs={{0,4},{4,8},{8,12},{12,16},{16,20},{20,24},{24,28},{1,5},{5,9},{9,... | collective-permute-start | bytes 393224 | tf_op jit(solution)/shard_map/while/body/eval_jaxpr/ppermute | solution.py:11
  77.5 1.0 fusion.53
  79.9 1.9 %multiply_add_fusion.5 = f32[2,8,256,128]{3,2,1,0:T(8,128)S(1)} fusion(f32[2,8,256,128]{3,2,1,0:T(8,128)S(1)} %get-tuple-element.382, f32[2,256,256,8]{2,1,3,0:T(8,128)S(1)} %get-tuple-element.362, f32[2,8,256]{2,1,0:T(8,128)S(1)} %max.9, pred[256,256]{0,1:T(8,128)(4,1)S(1)} %and_and_fusion.2, f32[2,8,256]{2,1,0:T(8,128)S(1)} %get-tuple-element.364, ...), kind=kOutput, calls=%fused_computation.7.clone.1 | convolution fusion | flops 274726912 | bytes 8617984 | tf_op jit(solution)/shard_map/while/body/eval_jaxpr/kgtp,pkd->kgtd/dot_general | solution.py:24
  81.8 4.2 %collective-permute-start = (s32[256]{0:T(256)S(1)}, s32[256]{0:T(256)S(1)}, u32[]{:S(2)}, u32[]{:S(2)}) collective-permute-start(s32[256]{0:T(256)S(1)} %get-tuple-element.385), channel_id=1, source_target_pairs={{0,4},{4,8},{8,12},{12,16},{16,20},{20,24},{24,28},{1,5},{5,9},{9,... | collective-permute-start | bytes 3080 | tf_op jit(solution)/shard_map/while/body/eval_jaxpr/ppermute | solution.py:11
  86.0 3.8 %collective-permute-start.1 = (bf16[256,2,128]{2,0,1:T(8,128)(2,1)}, bf16[256,2,128]{2,0,1:T(8,128)(2,1)S(1)}, u32[]{:S(2)}, u32[]{:S(2)}) collective-permute-start(bf16[256,2,128]{2,0,1:T(8,128)(2,1)} %get-tuple-element.383), channel_id=1, source_target_pairs={{0,4},{4,8},{8,12},{12,16},{16,20},{20,24},{24,28},{1,5},{5,9},{9,... | collective-permute-start | bytes 393224 | tf_op jit(solution)/shard_map/while/body/eval_jaxpr/ppermute | solution.py:11
  89.8 1.9 %collective-permute-start.2 = (bf16[256,2,128]{2,0,1:T(8,128)(2,1)}, bf16[256,2,128]{2,0,1:T(8,128)(2,1)S(1)}, u32[]{:S(2)}, u32[]{:S(2)}) collective-permute-start(bf16[256,2,128]{2,0,1:T(8,128)(2,1)} %get-tuple-element.384), channel_id=1, source_target_pairs={{0,4},{4,8},{8,12},{12,16},{16,20},{20,24},{24,28},{1,5},{5,9},{9,... | collective-permute-start | bytes 393224 | tf_op jit(solution)/shard_map/while/body/eval_jaxpr/ppermute | solution.py:11
  95.8 1.9 %multiply_add_fusion.5 = f32[2,8,256,128]{3,2,1,0:T(8,128)S(1)} fusion(f32[2,8,256,128]{3,2,1,0:T(8,128)S(1)} %get-tuple-element.382, f32[2,256,256,8]{2,1,3,0:T(8,128)S(1)} %get-tuple-element.362, f32[2,8,256]{2,1,0:T(8,128)S(1)} %max.9, pred[256,256]{0,1:T(8,128)(4,1)S(1)} %and_and_fusion.2, f32[2,8,256]{2,1,0:T(8,128)S(1)} %get-tuple-element.364, ...), kind=kOutput, calls=%fused_computation.7.clone.1 | convolution fusion | flops 274726912 | bytes 8617984 | tf_op jit(solution)/shard_map/while/body/eval_jaxpr/kgtp,pkd->kgtd/dot_general | solution.py:24
  99.9 17.0 %all_to_all.5 = bf16[4,64,2048]{2,1,0:T(8,128)(2,1)S(1)} all-to-all(bf16[4,64,2048]{2,1,0:T(8,128)(2,1)S(1)} %pad_maximum_fusion), channel_id=1, replica_groups=mesh['ctx'=8,'tp'=4] {'tp'}, dimensions={0} | all-to-all | bytes 2097152 | tf_op jit(solution)/shard_map/all_to_all | solution.py:78
  116.9 1.0 copy.45
  (84 shorter events, 20.1 us)
Async XLA Ops:
  4.7 4.7 %copy-start.1 = (bf16[256,2,128]{2,1,0:T(2,128)(2,1)S(1)}, bf16[256,2,128]{2,1,0:T(2,128)(2,1)}, u32[]{:S(2)}) copy-start(bf16[256,2,128]{2,1,0:T(2,128)(2,1)} %param.8) | copy-start | bytes 393220
  6.4 1.9 %copy-start = (f32[2,256,256,8]{2,1,3,0:T(8,128)}, f32[2,256,256,8]{2,1,3,0:T(8,128)S(1)}, u32[]{:S(2)}) copy-start(f32[2,256,256,8]{2,1,3,0:T(8,128)S(1)} %get-tuple-element.285) | copy-start | bytes 12582916
  10.0 3.4 %copy-start.2 = (s32[256]{0:T(256)S(1)}, s32[256]{0:T(256)}, u32[]{:S(2)}) copy-start(s32[256]{0:T(256)} %param.9) | copy-start | bytes 3076
  13.5 11.8 %collective-permute-start = (s32[256]{0:T(256)S(1)}, s32[256]{0:T(256)S(1)}, u32[]{:S(2)}, u32[]{:S(2)}) collective-permute-start(s32[256]{0:T(256)S(1)} %get-tuple-element.385), channel_id=1, source_target_pairs={{0,4},{4,8},{8,12},{12,16},{16,20},{20,24},{24,28},{1,5},{5,9},{9,... | collective-permute-start | bytes 3080 | tf_op jit(solution)/shard_map/while/body/eval_jaxpr/ppermute | solution.py:11
  18.4 7.1 %collective-permute-start.1 = (bf16[256,2,128]{2,0,1:T(8,128)(2,1)}, bf16[256,2,128]{2,0,1:T(8,128)(2,1)S(1)}, u32[]{:S(2)}, u32[]{:S(2)}) collective-permute-start(bf16[256,2,128]{2,0,1:T(8,128)(2,1)} %get-tuple-element.383), channel_id=1, source_target_pairs={{0,4},{4,8},{8,12},{12,16},{16,20},{20,24},{24,28},{1,5},{5,9},{9,... | collective-permute-start | bytes 393224 | tf_op jit(solution)/shard_map/while/body/eval_jaxpr/ppermute | solution.py:11
  21.8 6.2 %collective-permute-start.2 = (bf16[256,2,128]{2,0,1:T(8,128)(2,1)}, bf16[256,2,128]{2,0,1:T(8,128)(2,1)S(1)}, u32[]{:S(2)}, u32[]{:S(2)}) collective-permute-start(bf16[256,2,128]{2,0,1:T(8,128)(2,1)} %get-tuple-element.384), channel_id=1, source_target_pairs={{0,4},{4,8},{8,12},{12,16},{16,20},{20,24},{24,28},{1,5},{5,9},{9,... | collective-permute-start | bytes 393224 | tf_op jit(solution)/shard_map/while/body/eval_jaxpr/ppermute | solution.py:11
  30.6 11.2 %collective-permute-start = (s32[256]{0:T(256)S(1)}, s32[256]{0:T(256)S(1)}, u32[]{:S(2)}, u32[]{:S(2)}) collective-permute-start(s32[256]{0:T(256)S(1)} %get-tuple-element.385), channel_id=1, source_target_pairs={{0,4},{4,8},{8,12},{12,16},{16,20},{20,24},{24,28},{1,5},{5,9},{9,... | collective-permute-start | bytes 3080 | tf_op jit(solution)/shard_map/while/body/eval_jaxpr/ppermute | solution.py:11
  34.9 7.7 %collective-permute-start.1 = (bf16[256,2,128]{2,0,1:T(8,128)(2,1)}, bf16[256,2,128]{2,0,1:T(8,128)(2,1)S(1)}, u32[]{:S(2)}, u32[]{:S(2)}) collective-permute-start(bf16[256,2,128]{2,0,1:T(8,128)(2,1)} %get-tuple-element.383), channel_id=1, source_target_pairs={{0,4},{4,8},{8,12},{12,16},{16,20},{20,24},{24,28},{1,5},{5,9},{9,... | collective-permute-start | bytes 393224 | tf_op jit(solution)/shard_map/while/body/eval_jaxpr/ppermute | solution.py:11
  39.2 5.8 %collective-permute-start.2 = (bf16[256,2,128]{2,0,1:T(8,128)(2,1)}, bf16[256,2,128]{2,0,1:T(8,128)(2,1)S(1)}, u32[]{:S(2)}, u32[]{:S(2)}) collective-permute-start(bf16[256,2,128]{2,0,1:T(8,128)(2,1)} %get-tuple-element.384), channel_id=1, source_target_pairs={{0,4},{4,8},{8,12},{12,16},{16,20},{20,24},{24,28},{1,5},{5,9},{9,... | collective-permute-start | bytes 393224 | tf_op jit(solution)/shard_map/while/body/eval_jaxpr/ppermute | solution.py:11
  47.6 11.2 %collective-permute-start = (s32[256]{0:T(256)S(1)}, s32[256]{0:T(256)S(1)}, u32[]{:S(2)}, u32[]{:S(2)}) collective-permute-start(s32[256]{0:T(256)S(1)} %get-tuple-element.385), channel_id=1, source_target_pairs={{0,4},{4,8},{8,12},{12,16},{16,20},{20,24},{24,28},{1,5},{5,9},{9,... | collective-permute-start | bytes 3080 | tf_op jit(solution)/shard_map/while/body/eval_jaxpr/ppermute | solution.py:11
  51.8 7.6 %collective-permute-start.1 = (bf16[256,2,128]{2,0,1:T(8,128)(2,1)}, bf16[256,2,128]{2,0,1:T(8,128)(2,1)S(1)}, u32[]{:S(2)}, u32[]{:S(2)}) collective-permute-start(bf16[256,2,128]{2,0,1:T(8,128)(2,1)} %get-tuple-element.383), channel_id=1, source_target_pairs={{0,4},{4,8},{8,12},{12,16},{16,20},{20,24},{24,28},{1,5},{5,9},{9,... | collective-permute-start | bytes 393224 | tf_op jit(solution)/shard_map/while/body/eval_jaxpr/ppermute | solution.py:11
  56.6 5.3 %collective-permute-start.2 = (bf16[256,2,128]{2,0,1:T(8,128)(2,1)}, bf16[256,2,128]{2,0,1:T(8,128)(2,1)S(1)}, u32[]{:S(2)}, u32[]{:S(2)}) collective-permute-start(bf16[256,2,128]{2,0,1:T(8,128)(2,1)} %get-tuple-element.384), channel_id=1, source_target_pairs={{0,4},{4,8},{8,12},{12,16},{16,20},{20,24},{24,28},{1,5},{5,9},{9,... | collective-permute-start | bytes 393224 | tf_op jit(solution)/shard_map/while/body/eval_jaxpr/ppermute | solution.py:11
  64.4 11.4 %collective-permute-start = (s32[256]{0:T(256)S(1)}, s32[256]{0:T(256)S(1)}, u32[]{:S(2)}, u32[]{:S(2)}) collective-permute-start(s32[256]{0:T(256)S(1)} %get-tuple-element.385), channel_id=1, source_target_pairs={{0,4},{4,8},{8,12},{12,16},{16,20},{20,24},{24,28},{1,5},{5,9},{9,... | collective-permute-start | bytes 3080 | tf_op jit(solution)/shard_map/while/body/eval_jaxpr/ppermute | solution.py:11
  68.7 8.0 %collective-permute-start.1 = (bf16[256,2,128]{2,0,1:T(8,128)(2,1)}, bf16[256,2,128]{2,0,1:T(8,128)(2,1)S(1)}, u32[]{:S(2)}, u32[]{:S(2)}) collective-permute-start(bf16[256,2,128]{2,0,1:T(8,128)(2,1)} %get-tuple-element.383), channel_id=1, source_target_pairs={{0,4},{4,8},{8,12},{12,16},{16,20},{20,24},{24,28},{1,5},{5,9},{9,... | collective-permute-start | bytes 393224 | tf_op jit(solution)/shard_map/while/body/eval_jaxpr/ppermute | solution.py:11
  73.9 5.3 %collective-permute-start.2 = (bf16[256,2,128]{2,0,1:T(8,128)(2,1)}, bf16[256,2,128]{2,0,1:T(8,128)(2,1)S(1)}, u32[]{:S(2)}, u32[]{:S(2)}) collective-permute-start(bf16[256,2,128]{2,0,1:T(8,128)(2,1)} %get-tuple-element.384), channel_id=1, source_target_pairs={{0,4},{4,8},{8,12},{12,16},{16,20},{20,24},{24,28},{1,5},{5,9},{9,... | collective-permute-start | bytes 393224 | tf_op jit(solution)/shard_map/while/body/eval_jaxpr/ppermute | solution.py:11
  81.8 10.0 %collective-permute-start = (s32[256]{0:T(256)S(1)}, s32[256]{0:T(256)S(1)}, u32[]{:S(2)}, u32[]{:S(2)}) collective-permute-start(s32[256]{0:T(256)S(1)} %get-tuple-element.385), channel_id=1, source_target_pairs={{0,4},{4,8},{8,12},{12,16},{16,20},{20,24},{24,28},{1,5},{5,9},{9,... | collective-permute-start | bytes 3080 | tf_op jit(solution)/shard_map/while/body/eval_jaxpr/ppermute | solution.py:11
  86.0 6.6 %collective-permute-start.1 = (bf16[256,2,128]{2,0,1:T(8,128)(2,1)}, bf16[256,2,128]{2,0,1:T(8,128)(2,1)S(1)}, u32[]{:S(2)}, u32[]{:S(2)}) collective-permute-start(bf16[256,2,128]{2,0,1:T(8,128)(2,1)} %get-tuple-element.383), channel_id=1, source_target_pairs={{0,4},{4,8},{8,12},{12,16},{16,20},{20,24},{24,28},{1,5},{5,9},{9,... | collective-permute-start | bytes 393224 | tf_op jit(solution)/shard_map/while/body/eval_jaxpr/ppermute | solution.py:11
  89.8 5.3 %collective-permute-start.2 = (bf16[256,2,128]{2,0,1:T(8,128)(2,1)}, bf16[256,2,128]{2,0,1:T(8,128)(2,1)S(1)}, u32[]{:S(2)}, u32[]{:S(2)}) collective-permute-start(bf16[256,2,128]{2,0,1:T(8,128)(2,1)} %get-tuple-element.384), channel_id=1, source_target_pairs={{0,4},{4,8},{8,12},{12,16},{16,20},{20,24},{24,28},{1,5},{5,9},{9,... | collective-permute-start | bytes 393224 | tf_op jit(solution)/shard_map/while/body/eval_jaxpr/ppermute | solution.py:11
